TPU v7x, 32 devices: a whole 2x2x4 slice. The times are simulated.
32 devices in a mesh: dp: 2 (over core), fsdp: 16 (over z, y, x).
Axes of the slice: x: 2, y: 2, z: 4, core: 2. Of those that a mesh axis runs over, the one named last changes fastest.
Arguments:
- tokens: bfloat16 [8192, 4096], P(('dp', 'fsdp')), may hold values from -6 to 6
- block_codes: bfloat16 [256, 128, 128], P('fsdp'), may hold values from -4 to 4
- scales: float32 [256], P('fsdp'), may hold values from 0.008 to 0.03
- counts: int32 [16], replicated, may hold values from 0 to 16, as said below
- cotangent: bfloat16 [8192, 512], P(('dp', 'fsdp')), may hold values from -6 to 6
Outputs:
- projected: bfloat16 [8192, 512], P(('dp', 'fsdp'))
- token_grad: bfloat16 [8192, 4096], P(('dp', 'fsdp'))
- block_grad: bfloat16 [256, 128, 128], P('fsdp')
Inputs may be any that keep to these rules, and one draw needn't show every extreme that they name: counts sum to 128; each is at most 16, and some owner has exactly 16 and some none; slots past an owner's count hold values that are not used.
All inputs are finite; a program needn't handle non-finite values.
Results may differ from a plain program's by a relative error of at most 0.009.
Values may be sent and summed in bfloat16 or wider, within the bound.
A program may use at most 128 MiB of HBM per device.

v0:
```python
import functools
import math

import jax
import jax.numpy as jnp
from jax import lax
from jax.experimental import pallas as pl
from jax.experimental.pallas import tpu as pltpu
from jax.sharding import PartitionSpec as P

MESH = pl.DeviceIdType.MESH
F32 = jnp.float32
BF16 = jnp.bfloat16


def comm_kernel(
    outer, inner, q0, scale, counts_ref, scales_ref, codes_ref, tok_ref, cot_ref, proj_ref, tg_ref, out_ref,
    g_ref, held_ref, w_ref, acc_ref, pair_buf, wsend, wrecv, stage, sb0, sb1, ra1, rb1, ta, tb, ra2, rb2, fin, gsend, grecv,
    pair_sems, w_send, w_recv, x_send, x_recv, own_sems,
    gi_send, gi_recv, go_send, go_recv, fi_send, fi_recv, fo_send, fo_recv,
    ri_send, ri_recv, ro_send, ro_recv, out_sems,
):
    owners = outer * inner
    core = lax.axis_index("dp")
    other = 1 - core
    me = lax.axis_index("fsdp")
    o = me // inner
    i = me % inner
    slots, tile = codes_ref.shape[0], codes_ref.shape[1]
    even = stage.shape[0]
    half = tile // 2
    q1 = half - q0
    my_half = pl.ds(pl.multiple_of(core * half, half), half)
    parts = (pl.ds(0, q0), pl.ds(q0, q1))

    def rows(p):
        return pl.ds(pl.multiple_of(core * half + p * q0, q0), (q0, q1)[p])

    partner = (other, me)

    def mate_in(k):
        return (core, o * inner + (i + k) % inner)

    def mate_out(k):
        return (core, ((o + k) % outer) * inner + i)

    def mate(k):
        return (core, (me + k) % owners)

    def remote(src, dst, send, recv, device):
        return pltpu.make_async_remote_copy(
            src_ref=src, dst_ref=dst, send_sem=send, recv_sem=recv,
            device_id=device, device_id_type=MESH,
        )

    barrier = pltpu.get_barrier_semaphore()
    peers = [partner] + [mate(k) for k in range(1, owners)]
    for peer in peers:
        pl.semaphore_signal(barrier, inc=1, device_id=peer, device_id_type=MESH)
    pl.semaphore_wait(barrier, len(peers))

    started = []

    def go(copy):
        copy.start()
        started.append(copy)
        return copy

    offsets, ends, run, my_off, my_count = [], [], 0, 0, 0
    for d in range(owners):
        count = counts_ref[d]
        offsets.append(run)
        run = run + count
        ends.append(run)
        my_off = my_off + jnp.where(d < me, count, 0)
        my_count = my_count + jnp.where(d == me, count, 0)

    for k in range(owners):
        e = (me + k) % owners
        slot = jnp.minimum(lax.rem(e - my_off + even * owners, owners), slots - 1)
        block = (codes_ref[slot, my_half].astype(F32) * scales_ref[slot]).astype(BF16)
        if k == 0:
            wrecv[me] = block
        else:
            wsend[k] = block
    w_copies = [
        go(remote(wsend.at[k], wrecv.at[me], w_send.at[k], w_recv.at[k], mate(k)))
        for k in range(1, owners)
    ]

    depth = w_ref.shape[0]
    chunks = tok_ref.shape[1] // depth
    row_tiles, col_tiles = depth // tile, cot_ref.shape[1] // tile

    def terms(g, _):
        columns = pl.ds(pl.multiple_of(g * depth, depth), depth)
        part = lax.dot_general(
            tok_ref[:, columns], cot_ref[...], (((0,), (0,)), ((), ())), preferred_element_type=F32
        )
        part = (part * scale).astype(BF16)
        for r in range(row_tiles):
            for c in range(col_tiles):
                for h in range(2):
                    top = r * tile + h * half
                    g_ref[h, (g * row_tiles + r) * col_tiles + c] = part[
                        top : top + half, c * tile : (c + 1) * tile
                    ]
        return 0

    lax.fori_loop(0, chunks, terms, 0)
    pair = go(remote(g_ref.at[other], pair_buf, pair_sems.at[0], pair_sems.at[1], partner))

    for copy in w_copies:
        copy.wait_recv()
    for m in range(even):
        owner = 0
        for d in range(owners):
            owner = owner + jnp.where(ends[d] <= m * owners + me, 1, 0)
        block = wrecv[jnp.minimum(owner, owners - 1)]
        stage[m] = block
        held_ref[o, i, m, my_half] = block
    a1 = [
        go(remote(stage.at[:, parts[0]], held_ref.at[o, i, :, rows(0)],
                  gi_send.at[0, k], gi_recv.at[0, k], mate_in(k)))
        for k in range(1, inner)
    ]
    b1 = [
        go(remote(stage.at[:, parts[1]], held_ref.at[o, i, :, rows(1)],
                  go_send.at[0, k], go_recv.at[0, k], mate_out(k)))
        for k in range(1, outer)
    ]
    forwards = []

    def forward(src, place, send, recv):
        copy = remote(src, place, send, recv, partner)
        copy.start()
        forwards.append(copy)

    forward(stage, held_ref.at[o, i, :, my_half], own_sems.at[0], own_sems.at[1])

    pair.wait_recv()

    def build(s, _):
        oo, ii, m = s // (inner * even), (s // even) % inner, s % even
        b = m * owners + oo * inner + ii
        total = g_ref[core, b].astype(F32) + pair_buf[b].astype(F32)
        total = total.astype(BF16)
        sb0[oo, ii, m] = total[:q0]
        sb1[oo, ii, m] = total[q0:]
        return 0

    lax.fori_loop(0, owners * even, build, 0, unroll=4)

    ga1 = [
        go(remote(sb0.at[(o + k) % outer], ra1.at[k], ro_send.at[0, k], ro_recv.at[0, k], mate_out(k)))
        for k in range(1, outer)
    ]
    gb1 = [
        go(remote(sb1.at[:, (i + k) % inner], rb1.at[k], ri_send.at[0, k], ri_recv.at[0, k], mate_in(k)))
        for k in range(1, inner)
    ]

    for copy in a1:
        copy.wait_recv()
    a2 = [
        go(remote(held_ref.at[o, :, :, rows(0)], held_ref.at[o, :, :, rows(0)],
                  go_send.at[1, k], go_recv.at[1, k], mate_out(k)))
        for k in range(1, outer)
    ]
    for copy in b1:
        copy.wait_recv()
    b2 = [
        go(remote(held_ref.at[:, i, :, rows(1)], held_ref.at[:, i, :, rows(1)],
                  gi_send.at[1, k], gi_recv.at[1, k], mate_in(k)))
        for k in range(1, inner)
    ]
    for k in range(1, inner):
        place = held_ref.at[o, (i - k + inner) % inner, :, rows(0)]
        forward(place, place, fi_send.at[0, k], fi_recv.at[0, k])
    for k in range(1, outer):
        place = held_ref.at[(o - k + outer) % outer, i, :, rows(1)]
        forward(place, place, fo_send.at[0, k], fo_recv.at[0, k])

    for copy in ga1:
        copy.wait_recv()

    def sum_a(s, _):
        ii, m = s // even, s % even
        total = sb0[o, ii, m].astype(F32)
        for k in range(1, outer):
            total += ra1[k, ii, m].astype(F32)
        ta[ii, m] = total.astype(BF16)
        return 0

    lax.fori_loop(0, inner * even, sum_a, 0)
    ga2 = [
        go(remote(ta.at[(i + k) % inner], ra2.at[k], ri_send.at[1, k], ri_recv.at[1, k], mate_in(k)))
        for k in range(1, inner)
    ]
    for copy in gb1:
        copy.wait_recv()

    def sum_b(s, _):
        oo, m = s // even, s % even
        total = sb1[oo, i, m].astype(F32)
        for k in range(1, inner):
            total += rb1[k, oo, m].astype(F32)
        tb[oo, m] = total.astype(BF16)
        return 0

    lax.fori_loop(0, outer * even, sum_b, 0)
    gb2 = [
        go(remote(tb.at[(o + k) % outer], rb2.at[k], ro_send.at[1, k], ro_recv.at[1, k], mate_out(k)))
        for k in range(1, outer)
    ]

    for k, copy in enumerate(a2, 1):
        copy.wait_recv()
        place = held_ref.at[(o - k + outer) % outer, :, :, rows(0)]
        forward(place, place, fo_send.at[1, k], fo_recv.at[1, k])
    for k, copy in enumerate(b2, 1):
        copy.wait_recv()
        place = held_ref.at[:, (i - k + inner) % inner, :, rows(1)]
        forward(place, place, fi_send.at[1, k], fi_recv.at[1, k])

    for copy in ga2 + gb2:
        copy.wait_recv()
    for m in range(even):
        total = ta[i, m].astype(F32)
        for k in range(1, inner):
            total += ra2[k, m].astype(F32)
        fin[m, parts[0]] = total.astype(BF16)
        total = tb[o, m].astype(F32)
        for k in range(1, outer):
            total += rb2[k, m].astype(F32)
        fin[m, parts[1]] = total.astype(BF16)
    for k in range(owners):
        d = (me + k) % owners
        start = 0
        for x in range(owners):
            start = start + jnp.where(x < d, counts_ref[x], 0)
        m = jnp.minimum(lax.div(start - me + owners - 1, owners), even - 1)
        if k == 0:
            grecv[me] = fin[m]
        else:
            gsend[k] = fin[m]
    x_copies = [
        go(remote(gsend.at[k], grecv.at[me], x_send.at[k], x_recv.at[k], mate(k)))
        for k in range(1, owners)
    ]

    for copy in forwards:
        copy.wait_recv()
    acc_ref[...] = jnp.zeros_like(acc_ref)

    def products(g, _):
        columns = pl.ds(pl.multiple_of(g * depth, depth), depth)
        for r in range(row_tiles):
            for c in range(col_tiles):
                b = (g * row_tiles + r) * col_tiles + c
                e, m = b % owners, b // owners
                w_ref[r * tile : (r + 1) * tile, c * tile : (c + 1) * tile] = held_ref[e // inner, e % inner, m]
        weight = w_ref[...]
        acc_ref[...] += jnp.dot(tok_ref[:, columns], weight, preferred_element_type=F32)
        tg_ref[:, columns] = lax.dot_general(
            cot_ref[...], weight, (((1,), (1,)), ((), ())), preferred_element_type=F32
        ).astype(BF16)
        return 0

    lax.fori_loop(0, chunks, products, 0)
    proj_ref[...] = acc_ref[...].astype(BF16)

    for copy in x_copies:
        copy.wait_recv()
    for j in range(slots):
        used = jnp.where(j < my_count, 1.0, 0.0).astype(F32)
        block = grecv[lax.rem(my_off + j, owners)].astype(F32)
        out_ref[j, my_half] = (block * used).astype(BF16)
    place = out_ref.at[:, my_half]
    swap = remote(place, place, out_sems.at[0], out_sems.at[1], partner)
    swap.start()
    for copy in started:
        copy.wait_send()
    for copy in forwards:
        copy.wait_send()
    swap.wait()


def body(tokens, block_codes, scales, counts, cotangent):
    owners_total = lax.axis_size("fsdp")
    most_slots, tile = block_codes.shape[0], block_codes.shape[1]
    local_tokens, width = tokens.shape
    key_width = cotangent.shape[1]
    row_tiles, col_tiles = width // tile, key_width // tile
    block_count = row_tiles * col_tiles
    total_tokens = local_tokens * lax.axis_size("dp") * owners_total
    loss_scale = 1.0 / math.sqrt(total_tokens)
    inner = 4 if owners_total % 4 == 0 else 1
    outer = owners_total // inner
    even = block_count // owners_total
    half = tile // 2
    q0 = tile // 8
    q1 = half - q0
    assert even * owners_total == block_count and most_slots <= owners_total

    chunks = 8
    depth = width // chunks
    dma = pltpu.SemaphoreType.DMA
    vmem = pl.BlockSpec(memory_space=pltpu.VMEM)
    smem = pl.BlockSpec(memory_space=pltpu.SMEM)
    pairs_in, pairs_out = dma((2, inner)), dma((2, outer))
    return tuple(pl.pallas_call(
        functools.partial(comm_kernel, outer, inner, q0, loss_scale),
        in_specs=[smem, smem, vmem, vmem, vmem],
        out_specs=[vmem, vmem, vmem],
        out_shape=[
            jax.ShapeDtypeStruct((local_tokens, key_width), BF16),
            jax.ShapeDtypeStruct((local_tokens, width), BF16),
            jax.ShapeDtypeStruct((most_slots, tile, tile), BF16),
        ],
        scratch_shapes=[
            pltpu.VMEM((2, block_count, half, tile), BF16),
            pltpu.VMEM((outer, inner, even, tile, tile), BF16),
            pltpu.VMEM((depth, key_width), BF16),
            pltpu.VMEM((local_tokens, key_width), F32),
            pltpu.VMEM((block_count, half, tile), BF16),
            pltpu.VMEM((owners_total, half, tile), BF16),
            pltpu.VMEM((owners_total, half, tile), BF16),
            pltpu.VMEM((even, half, tile), BF16),
            pltpu.VMEM((outer, inner, even, q0, tile), BF16),
            pltpu.VMEM((outer, inner, even, q1, tile), BF16),
            pltpu.VMEM((outer, inner, even, q0, tile), BF16),
            pltpu.VMEM((inner, outer, even, q1, tile), BF16),
            pltpu.VMEM((inner, even, q0, tile), BF16),
            pltpu.VMEM((outer, even, q1, tile), BF16),
            pltpu.VMEM((inner, even, q0, tile), BF16),
            pltpu.VMEM((outer, even, q1, tile), BF16),
            pltpu.VMEM((even, half, tile), BF16),
            pltpu.VMEM((owners_total, half, tile), BF16),
            pltpu.VMEM((owners_total, half, tile), BF16),
            dma((2,)),
            dma((owners_total,)), dma((owners_total,)), dma((owners_total,)), dma((owners_total,)),
            dma((2,)),
            pairs_in, pairs_in, pairs_out, pairs_out,
            pairs_in, pairs_in, pairs_out, pairs_out,
            pairs_in, pairs_in, pairs_out, pairs_out,
            dma((2,)),
        ],
        compiler_params=pltpu.CompilerParams(
            collective_id=0, has_side_effects=True, vmem_limit_bytes=48 * 1024 * 1024
        ),
    )(counts, scales, block_codes, tokens, cotangent))


def solution(mesh):
    return jax.shard_map(
        body,
        mesh=mesh,
        in_specs=(
            P(("dp", "fsdp"), None),
            P("fsdp", None, None),
            P("fsdp"),
            P(),
            P(("dp", "fsdp"), None),
        ),
        out_specs=(P(("dp", "fsdp"), None), P(("dp", "fsdp"), None), P("fsdp", None, None)),
        check_vma=False,
    )
```

profile of v0, /device:TPU:0, one launch (start us, length us, event | category | flops | bytes accessed | tf_op | source)
XLA Modules:
  0.0 72.9 jit_solution(7106069540832638963)
XLA Ops:
  0.6 0.0 copy-start
  0.6 1.6 %copy-done = bf16[256,4096]{1,0:T(8,128)(2,1)S(1)} copy-done((bf16[256,4096]{1,0:T(8,128)(2,1)S(1)}, bf16[256,4096]{1,0:T(8,128)(2,1)}, u32[]{:S(2)}) %copy-start) | copy-done | bytes 2097176
  2.2 0.0 copy-start.1
  2.2 1.0 %copy-done.1 = bf16[16,128,128]{2,1,0:T(8,128)(2,1)S(1)} copy-done((bf16[16,128,128]{2,1,0:T(8,128)(2,1)S(1)}, bf16[16,128,128]{2,1,0:T(8,128)(2,1)}, u32[]{:S(2)}) %copy-start.1) | copy-done | bytes 524312
  3.3 0.0 copy-start.2
  3.3 0.9 %copy-done.2 = bf16[256,512]{1,0:T(8,128)(2,1)S(1)} copy-done((bf16[256,512]{1,0:T(8,128)(2,1)S(1)}, bf16[256,512]{1,0:T(8,128)(2,1)}, u32[]{:S(2)}) %copy-start.2) | copy-done | bytes 262168
  4.2 0.0 copy-start.3
  4.2 0.7 copy-done.3
  4.9 0.0 copy-start.4
  4.9 0.7 copy-done.4
  5.5 64.5 %shard_map.76 = (bf16[256,512]{1,0:T(8,128)(2,1)S(1)}, bf16[256,4096]{1,0:T(8,128)(2,1)S(1)}, bf16[16,128,128]{2,1,0:T(8,128)(2,1)S(1)}) custom-call(s32[16]{0:T(128)S(1)} %copy-done.3, f32[16]{0:T(128)S(1)} %copy-done.4, bf16[16,128,128]{2,1,0:T(8,128)(2,1)S(1)} %copy-done.1, bf16[256,4096]{1,0:T(8,128)(2,1)S(1)} %copy-done, bf16[256,512]{1,0:T(8,128)(2,1)S(1)} %copy-done.2), custom_call_target="tpu_custom_call" | custom-call | tf_op jit(solution)/shard_map/pallas_call | solution.py:312
  70.0 0.7 copy.11
  70.7 1.3 %copy.12 = bf16[256,4096]{1,0:T(8,128)(2,1)} copy(bf16[256,4096]{1,0:T(8,128)(2,1)S(1)} %get-tuple-element.7) | data formatting | bytes 4194304
  72.1 0.8 %copy.13 = bf16[16,128,128]{2,1,0:T(8,128)(2,1)} copy(bf16[16,128,128]{2,1,0:T(8,128)(2,1)S(1)} %get-tuple-element.8) | data formatting | bytes 1048576
Async XLA Ops:
  0.6 1.6 %copy-start = (bf16[256,4096]{1,0:T(8,128)(2,1)S(1)}, bf16[256,4096]{1,0:T(8,128)(2,1)}, u32[]{:S(2)}) copy-start(bf16[256,4096]{1,0:T(8,128)(2,1)} %tok_ref.1) | copy-start | bytes 6291460
  2.2 1.0 %copy-start.1 = (bf16[16,128,128]{2,1,0:T(8,128)(2,1)S(1)}, bf16[16,128,128]{2,1,0:T(8,128)(2,1)}, u32[]{:S(2)}) copy-start(bf16[16,128,128]{2,1,0:T(8,128)(2,1)} %codes_ref.1) | copy-start | bytes 1572868
  3.3 0.9 %copy-start.2 = (bf16[256,512]{1,0:T(8,128)(2,1)S(1)}, bf16[256,512]{1,0:T(8,128)(2,1)}, u32[]{:S(2)}) copy-start(bf16[256,512]{1,0:T(8,128)(2,1)} %cot_ref.1) | copy-start | bytes 786436
  4.2 0.7 copy-start.3
  4.9 0.7 copy-start.4
where the time goes:
time: 73.1 us; the launch traced here: 72.9 us
  Pallas kernels  64.5 us (88%)
  local copies, waits for them, and re-layouts  7.7 us (11%)
    pallas_call x1, Pallas kernels, body(): pl.pallas_call(functools.partial(comm_kernel, outer, inner, q0, loss_scal...  64.5 us
    unnamed x13, local copies, waits for them, and re-layouts  7.7 us

commit v1 on v0

v1 whole, which is shorter than its diff:
```python
import functools
import math
import types

import jax
import jax.numpy as jnp
from jax import lax
from jax.experimental import pallas as pl
from jax.experimental.pallas import tpu as pltpu
from jax.sharding import PartitionSpec as P

MESH = pl.DeviceIdType.MESH
F32 = jnp.float32
BF16 = jnp.bfloat16

PLANE = 4
CORES = 2
GROUP = PLANE * CORES
CHUNKS = 4


def kernel(names, owners, slots, scale, *refs):
    r = types.SimpleNamespace(**dict(zip(names, refs)))
    planes = owners // PLANE
    h = lax.axis_index("dp")
    me = lax.axis_index("fsdp")
    z, c = me // PLANE, me % PLANE
    y, x = c // 2, c % 2
    oy, ox = 1 - y, 1 - x
    most, tile = r.codes_v.shape[0], r.codes_v.shape[1]
    span = r.own_v.shape[1]
    part = span // 2
    places = CHUNKS * span
    blocks = places * GROUP
    period = GROUP * slots
    chunk_blocks = span * GROUP
    plane_most = PLANE * most
    width = r.tok_v.shape[2]
    first, last = pl.ds(0, part), pl.ds(part, span - part)

    x_dev = (h, z * PLANE + 2 * y + ox)
    y_dev = (h, z * PLANE + 2 * oy + x)
    d_dev = (h, z * PLANE + 2 * oy + ox)
    partner = (1 - h, me)

    def z_dev(d):
        return (h, ((z + 1 - 2 * d + planes) % planes) * PLANE + c)

    def remote(src, dst, send, recv, device):
        return pltpu.make_async_remote_copy(
            src_ref=src, dst_ref=dst, send_sem=send, recv_sem=recv, device_id=device, device_id_type=MESH
        )

    ends = []

    def guarded(conditions, act):
        if conditions:
            pl.when(conditions[0])(lambda: guarded(conditions[1:], act))
        else:
            act()

    def go(copy, when=()):
        guarded(when, copy.start)
        ends.append(lambda: guarded(when, copy.wait_send))
        return copy

    local = [
        pltpu.make_async_copy(r.counts_h, r.counts_s, r.in_sems.at[0]),
        pltpu.make_async_copy(r.scales_h, r.scales_s, r.in_sems.at[1]),
        pltpu.make_async_copy(r.codes_h, r.codes_v, r.in_sems.at[2]),
        pltpu.make_async_copy(r.cot_h, r.cot_v, r.in_sems.at[3]),
    ]
    tok_in = [
        pltpu.make_async_copy(
            r.tok_h.at[:, pl.ds(k * width, width)], r.tok_v.at[k], r.tok_sems.at[k]
        )
        for k in range(CHUNKS)
    ]
    for copy in local + tok_in:
        copy.start()

    barrier = pltpu.get_barrier_semaphore()
    for peer in (x_dev, y_dev, d_dev, partner):
        pl.semaphore_signal(barrier, inc=1, device_id=peer, device_id_type=MESH)
    has_up, has_down = z < planes - 1, z > 0

    @pl.when(has_up)
    def _():
        pl.semaphore_signal(barrier, inc=1, device_id=z_dev(0), device_id_type=MESH)

    @pl.when(has_down)
    def _():
        pl.semaphore_signal(barrier, inc=1, device_id=z_dev(1), device_id_type=MESH)

    for copy in local[:3]:
        copy.wait()
    pl.semaphore_wait(barrier, 4 + jnp.where(has_up, 1, 0) + jnp.where(has_down, 1, 0))

    base, run = 0, [0] * PLANE
    for d in range(owners):
        count = r.counts_s[d]
        base = base + jnp.where(d < z * PLANE, count, 0)
        run[d % PLANE] = run[d % PLANE] + jnp.where(d // PLANE == z, count, 0)
    starts = [base]
    for i in range(PLANE):
        starts.append(starts[-1] + run[i])
    plane_end = starts[PLANE]

    def pick(values, index):
        total = values[0]
        for i in range(1, len(values)):
            total = jnp.where(index == i, values[i], total)
        return total

    my_off = pick(starts[:PLANE], c)
    my_count = pick(run, c)

    p = (2 * z) // planes

    def far_chunk(j):
        return (j + (CHUNKS // 2) * (1 - p)) % CHUNKS

    def near_chunk(j):
        return (j + (CHUNKS // 2) * p) % CHUNKS

    behind = (z, planes - 1 - z)

    def ahead(d, q):
        return q if d == 0 else CHUNKS - 1 - q

    def w_has_recv(d, q):
        return (ahead(d, q) * chunk_blocks < behind[d] * plane_most,)

    def w_has_send(d, q):
        v = behind[d]
        return (v < planes - 1, ahead(d, q) * chunk_blocks < (v + 1) * plane_most)

    def g_has_recv(d, q):
        v = behind[d]
        return (v > 0, ahead(d, CHUNKS - 1 - q) * chunk_blocks < (planes - v) * plane_most)

    def g_has_send(d, q):
        return (ahead(d, CHUNKS - 1 - q) * chunk_blocks < (planes - 1 - behind[d]) * plane_most,)

    def place_block(q, i):
        return (q * span + i) * GROUP + h * PLANE + c

    mates = [(y, x), (y, ox), (oy, x), (oy, ox)]
    mate_devs = [None, x_dev, y_dev, d_dev]

    def scatter():
        for k, (ty, tx) in enumerate(mates):
            target = 2 * ty + tx
            for s in range(slots):
                t = lax.rem(s * GROUP + h * PLANE + target - my_off + blocks, period)
                t = jnp.minimum(t, most - 1)
                block = (r.codes_v[t].astype(F32) * r.scales_s[t]).astype(BF16)
                if k == 0:
                    r.sc_recv[c, s] = block
                else:
                    r.sc_send[k, s] = block
        for k in range(1, PLANE):
            go(scatter_copy(k))

    def scatter_copy(k):
        return remote(r.sc_send.at[k], r.sc_recv.at[c], r.sc_sems.at[0, k], r.sc_sems.at[1, k], mate_devs[k])

    def gather_own():
        for k in range(1, PLANE):
            scatter_copy(k).wait_recv()
        for i in range(PLANE):
            r.sc_loc[i * slots : (i + 1) * slots] = r.sc_recv[i]
        for q in range(CHUNKS):
            for i in range(span):
                b = place_block(q, i)
                owner = 0
                for e in starts[1:PLANE]:
                    owner = owner + jnp.where(b >= e, 1, 0)
                r.own_v[q, i] = r.sc_loc[owner * slots + (q * span + i) % slots]

    def w_task(d, q, when):
        copy = remote(r.w_send.at[d, q], r.w_recv.at[d, q], r.wz_sems.at[0, d, q], r.wz_sems.at[1, d, q], z_dev(d))

        guarded(when + w_has_recv(d, q), copy.wait_recv)

        def merge():
            for i in range(span):
                b = place_block(q, i)
                other = b < base if d == 0 else b >= plane_end
                r.w_send[d, q, i] = jnp.where(other, r.w_recv[d, q, i], r.own_v[q, i])

        sends = when + w_has_send(d, q)
        guarded(sends, merge)
        go(copy, sends)

    def line_order(d, j):
        return (j + CHUNKS // 2) % CHUNKS if d == 0 else j

    def w_primary(j):
        for d in range(2):
            w_task(d, line_order(d, (j + CHUNKS // 2) % CHUNKS), (behind[d] == 0,))
            w_task(d, line_order(d, j), (p == d, behind[d] > 0))

    def w_secondary(j):
        for d in range(2):
            w_task(d, line_order(d, j), (p == 1 - d,))

    def push(place, k, j):
        return remote(place, place, r.fw_sems.at[0, k, j], r.fw_sems.at[1, k, j], partner)

    def gather_copy(place, k, j, device):
        return remote(place, place, r.ag_sems.at[0, k, j], r.ag_sems.at[1, k, j], device)

    def w_final(j):
        q = near_chunk(j)
        w_secondary(j)
        for i in range(span):
            b = place_block(q, i)
            r.w_all[h, q, y, x, i] = jnp.where(
                b < base, r.w_recv[0, q, i], jnp.where(b >= plane_end, r.w_recv[1, q, i], r.own_v[q, i])
            )
        place = r.w_all.at[h, q, y, x]
        go(gather_copy(place, 0, j, x_dev))
        go(gather_copy(place, 1, j, y_dev))
        go(push(place, 0, j))

    def w_forward(j):
        q = near_chunk(j)
        place = r.w_all.at[h, q, y, ox]
        gather_copy(place, 0, j, x_dev).wait_recv()
        go(gather_copy(r.w_all.at[h, q, y, ox, first], 2, j, y_dev))
        go(push(place, 1, j))
        place = r.w_all.at[h, q, oy, x]
        gather_copy(place, 1, j, y_dev).wait_recv()
        go(gather_copy(r.w_all.at[h, q, oy, x, last], 3, j, x_dev))
        go(push(place, 2, j))

    def w_diagonal(j):
        q = near_chunk(j)
        gather_copy(r.w_all.at[h, q, oy, ox, first], 2, j, y_dev).wait_recv()
        gather_copy(r.w_all.at[h, q, oy, ox, last], 3, j, x_dev).wait_recv()
        go(push(r.w_all.at[h, q, oy, ox], 3, j))

    depth = r.w_mat.shape[0]
    row_tiles = depth // tile

    def products(j):
        q = near_chunk(j)
        for k, (ty, tx) in enumerate(mates):
            push(r.w_all.at[1 - h, q, ty, tx], k, j).wait_recv()
        for rr in range(row_tiles):
            for cc in range(PLANE):
                r.w_mat[rr * tile : (rr + 1) * tile, cc * tile : (cc + 1) * tile] = r.w_all[
                    rr % CORES, q, cc // 2, cc % 2, rr // CORES
                ]
        weight = r.w_mat[...]
        term = jnp.dot(r.tok_v[q], weight, preferred_element_type=F32)
        if j == 0:
            r.acc[...] = term
        elif j < CHUNKS - 1:
            r.acc[...] += term
        else:
            r.proj[...] = (r.acc[...] + term).astype(BF16)
        r.tg[:, pl.ds(pl.multiple_of(q * depth, depth), depth)] = lax.dot_general(
            r.cot_v[...], weight, (((1,), (1,)), ((), ())), preferred_element_type=F32
        ).astype(BF16)

    steps = 2
    sub = depth // steps

    def pair_copy(j):
        q = far_chunk(j)
        return remote(r.g_terms.at[1 - h, q], r.g_pair.at[q], r.pair_sems.at[0, j], r.pair_sems.at[1, j], partner)

    def terms(j):
        q = far_chunk(j)
        for g in range(steps):
            value = lax.dot_general(
                r.tok_v[q, :, g * sub : (g + 1) * sub], r.cot_v[...], (((0,), (0,)), ((), ())),
                preferred_element_type=F32,
            )
            value = (value * scale).astype(BF16)
            for rr in range(sub // tile):
                row = g * (sub // tile) + rr
                for cc in range(PLANE):
                    r.g_terms[row % CORES, q, cc // 2, cc % 2, row // CORES] = value[
                        rr * tile : (rr + 1) * tile, cc * tile : (cc + 1) * tile
                    ]
        go(pair_copy(j))

    def pair_sum(j):
        q = far_chunk(j)
        pair_copy(j).wait_recv()

        for a in range(2):
            for b in range(2):
                r.g_sum[q, a, b] = (r.g_terms[h, q, a, b].astype(F32) + r.g_pair[q, a, b].astype(F32)).astype(BF16)

    def rs_one(j):
        q = far_chunk(j)
        return [
            remote(r.g_sum.at[q, oy, :, first], r.r1a.at[q], r.rs_sems.at[0, 0, j], r.rs_sems.at[1, 0, j], y_dev),
            remote(r.g_sum.at[q, :, ox, last], r.r1b.at[q], r.rs_sems.at[0, 1, j], r.rs_sems.at[1, 1, j], x_dev),
        ]

    def rs_two(j):
        q = far_chunk(j)
        return [
            remote(r.s2a.at[q], r.r2a.at[q], r.rs_sems.at[0, 2, j], r.rs_sems.at[1, 2, j], x_dev),
            remote(r.s2b.at[q], r.r2b.at[q], r.rs_sems.at[0, 3, j], r.rs_sems.at[1, 3, j], y_dev),
        ]

    def reduce_one(j):
        for copy in rs_one(j):
            go(copy)

    def reduce_two(j):
        q = far_chunk(j)
        one, two = rs_one(j), rs_two(j)
        one[0].wait_recv()
        r.s2a[q] = (r.g_sum[q, y, ox, first].astype(F32) + r.r1a[q, ox].astype(F32)).astype(BF16)
        go(two[0])
        one[1].wait_recv()
        r.s2b[q] = (r.g_sum[q, oy, x, last].astype(F32) + r.r1b[q, oy].astype(F32)).astype(BF16)
        go(two[1])

    def plane_sum(j):
        q = far_chunk(j)
        two = rs_two(j)
        two[0].wait_recv()
        r.g_plane[q, first] = (
            r.g_sum[q, y, x, first].astype(F32) + r.r1a[q, x].astype(F32) + r.r2a[q].astype(F32)
        )
        two[1].wait_recv()
        r.g_plane[q, last] = (
            r.g_sum[q, y, x, last].astype(F32) + r.r1b[q, y].astype(F32) + r.r2b[q].astype(F32)
        )

    def behind_sum(d, q):
        return jnp.where(behind[d] > 0, r.gz_recv[d, q].astype(F32), 0.0)

    def g_task(d, q, when):
        copy = remote(r.gz_send.at[d, q], r.gz_recv.at[d, q], r.gz_sems.at[0, d, q], r.gz_sems.at[1, d, q], z_dev(d))

        guarded(when + g_has_recv(d, q), copy.wait_recv)

        def add():
            r.gz_send[d, q] = (r.g_plane[q] + behind_sum(d, q)).astype(BF16)

        sends = when + g_has_send(d, q)
        guarded(sends, add)
        go(copy, sends)

    def g_primary(slot):
        for d in range(2):
            if slot < CHUNKS:
                g_task(d, line_order(d, slot), (behind[d] == 0,))
            if slot > 0:
                g_task(d, line_order(d, slot - 1), (p == d, behind[d] > 0))

    def g_secondary(j):
        for d in range(2):
            g_task(d, line_order(d, j), (p == 1 - d,))
        q = near_chunk(j)
        r.g_full[pl.ds(q * span, span)] = (r.g_plane[q] + behind_sum(0, q) + behind_sum(1, q)).astype(BF16)

    def owner_copy(k):
        return remote(r.fs_send.at[k], r.fs_all.at[h, c], r.fs_sems.at[0, k], r.fs_sems.at[1, k], mate_devs[k])

    def give(k):
        ty, tx = mates[k]
        place = r.fs_all.at[h, 2 * ty + tx]
        return remote(place, place, r.fp_sems.at[0, k], r.fp_sems.at[1, k], partner)

    def to_owners():
        for k in (3, 1, 2, 0):
            ty, tx = mates[k]
            off = pick(starts[:PLANE], 2 * ty + tx)
            for s in range(slots):
                t = lax.rem(s * GROUP + h * PLANE + c - off + blocks, period)
                m = jnp.minimum(lax.div(off + t, GROUP), places - 1)
                block = r.g_full[m]
                if k == 0:
                    r.fs_all[h, c, s] = block
                else:
                    r.fs_send[k, s] = block
        for k in (3, 1, 2):
            go(owner_copy(k))
        go(give(0))

    def finish():
        for k in (1, 2, 3):
            owner_copy(k).wait_recv()
            go(give(k))
        for k in range(PLANE):
            ty, tx = mates[k]
            place = r.fs_all.at[1 - h, 2 * ty + tx]
            remote(place, place, r.fp_sems.at[0, k], r.fp_sems.at[1, k], partner).wait_recv()
        for k in range(CORES * PLANE):
            r.fs_loc[k * slots : (k + 1) * slots] = r.fs_all[k // PLANE, k % PLANE]
        for j in range(most):
            b = my_off + j
            block = r.fs_loc[lax.rem(b, GROUP) * slots + lax.rem(lax.div(b, GROUP), slots)]
            r.out[j] = jnp.where(j < my_count, block, jnp.zeros_like(block))

    scatter()
    local[3].wait()
    for copy in tok_in:
        copy.wait()
    for j in range(CHUNKS):
        terms(j)
    pair_sum(0)
    reduce_one(0)
    pair_sum(1)
    reduce_one(1)
    gather_own()
    w_primary(0)
    w_primary(1)
    pair_sum(2)
    pair_sum(3)
    reduce_two(0)
    reduce_one(2)
    w_primary(2)
    reduce_two(1)
    reduce_one(3)
    plane_sum(0)
    g_primary(0)
    w_primary(3)
    w_final(0)
    reduce_two(2)
    plane_sum(1)
    g_primary(1)
    w_final(1)
    w_forward(0)
    reduce_two(3)
    plane_sum(2)
    g_primary(2)
    w_final(2)
    w_forward(1)
    w_diagonal(0)
    plane_sum(3)
    g_primary(3)
    w_final(3)
    g_primary(4)
    g_secondary(0)
    w_forward(2)
    w_diagonal(1)
    products(0)
    g_secondary(1)
    w_forward(3)
    g_secondary(2)
    g_secondary(3)
    to_owners()
    w_diagonal(2)
    products(1)
    w_diagonal(3)
    products(2)
    finish()
    products(3)
    for end in ends:
        end()


def body(tokens, block_codes, scales, counts, cotangent):
    owners = lax.axis_size("fsdp")
    most, tile = block_codes.shape[0], block_codes.shape[1]
    local_tokens, width = tokens.shape
    key_width = cotangent.shape[1]
    blocks = (width // tile) * (key_width // tile)
    total_tokens = local_tokens * lax.axis_size("dp") * owners
    slots = -(-most // GROUP)
    span = blocks // (GROUP * CHUNKS)
    depth = width // CHUNKS
    assert lax.axis_size("dp") == CORES and owners % PLANE == 0 and key_width == PLANE * tile
    assert span * GROUP * CHUNKS == blocks and span % 2 == 0 and span % slots == 0

    dma = pltpu.SemaphoreType.DMA
    vmem = pl.BlockSpec(memory_space=pltpu.VMEM)
    hbm = pl.BlockSpec(memory_space=pltpu.HBM)

    def held(*shape, kind=BF16):
        return pltpu.VMEM(shape + (tile, tile), kind)

    half, places = span // 2, span * CHUNKS
    scratch = {
        "counts_s": pltpu.SMEM(counts.shape, jnp.int32),
        "scales_s": pltpu.SMEM(scales.shape, F32),
        "codes_v": pltpu.VMEM(block_codes.shape, BF16),
        "cot_v": pltpu.VMEM(cotangent.shape, BF16),
        "tok_v": pltpu.VMEM((CHUNKS, local_tokens, depth), BF16),
        "sc_send": held(PLANE, slots),
        "sc_recv": held(PLANE, slots),
        "sc_loc": held(PLANE * slots),
        "fs_loc": held(CORES * PLANE * slots),
        "own_v": held(CHUNKS, span),
        "w_send": held(2, CHUNKS, span),
        "w_recv": held(2, CHUNKS, span),
        "w_all": held(CORES, CHUNKS, 2, 2, span),
        "w_mat": pltpu.VMEM((depth, key_width), BF16),
        "acc": pltpu.VMEM((local_tokens, key_width), F32),
        "g_terms": held(CORES, CHUNKS, 2, 2, span),
        "g_pair": held(CHUNKS, 2, 2, span),
        "g_sum": held(CHUNKS, 2, 2, span),
        "r1a": held(CHUNKS, 2, half),
        "r1b": held(CHUNKS, 2, half),
        "s2a": held(CHUNKS, half),
        "s2b": held(CHUNKS, half),
        "r2a": held(CHUNKS, half),
        "r2b": held(CHUNKS, half),
        "g_plane": held(CHUNKS, span, kind=F32),
        "gz_send": held(2, CHUNKS, span),
        "gz_recv": held(2, CHUNKS, span),
        "g_full": held(places),
        "fs_send": held(PLANE, slots),
        "fs_all": held(CORES, PLANE, slots),
        "in_sems": dma((4,)),
        "tok_sems": dma((CHUNKS,)),
        "sc_sems": dma((2, PLANE)),
        "wz_sems": dma((2, 2, CHUNKS)),
        "ag_sems": dma((2, 4, CHUNKS)),
        "fw_sems": dma((2, 4, CHUNKS)),
        "pair_sems": dma((2, CHUNKS)),
        "rs_sems": dma((2, 4, CHUNKS)),
        "gz_sems": dma((2, 2, CHUNKS)),
        "fs_sems": dma((2, PLANE)),
        "fp_sems": dma((2, PLANE)),
    }
    names = ["counts_h", "scales_h", "codes_h", "tok_h", "cot_h", "proj", "tg", "out"] + list(scratch)
    return tuple(pl.pallas_call(
        functools.partial(kernel, names, owners, slots, 1.0 / math.sqrt(total_tokens)),
        in_specs=[hbm] * 5,
        out_specs=[vmem, vmem, vmem],
        out_shape=[
            jax.ShapeDtypeStruct((local_tokens, key_width), BF16),
            jax.ShapeDtypeStruct((local_tokens, width), BF16),
            jax.ShapeDtypeStruct((most, tile, tile), BF16),
        ],
        scratch_shapes=list(scratch.values()),
        compiler_params=pltpu.CompilerParams(
            collective_id=0, has_side_effects=True, vmem_limit_bytes=56 * 1024 * 1024
        ),
    )(counts, scales, block_codes, tokens, cotangent))


def solution(mesh):
    return jax.shard_map(
        body,
        mesh=mesh,
        in_specs=(
            P(("dp", "fsdp"), None),
            P("fsdp", None, None),
            P("fsdp"),
            P(),
            P(("dp", "fsdp"), None),
        ),
        out_specs=(P(("dp", "fsdp"), None), P(("dp", "fsdp"), None), P("fsdp", None, None)),
        check_vma=False,
    )
```

time: 73.1 us -> 61.1 us (0.84); the launches traced: 72.9 us -> 59.9 us
  Pallas kernels: 64.5 us -> 53.6 us
  local copies, waits for them, and re-layouts: 7.7 us -> 5.65 us
    pallas_call x1, Pallas kernels: 64.5 us -> 53.6 us  [body(): pl.pallas_call(functools.partial(kernel, names, owners, slots, 1.0 / math...]
    unnamed x13 -> x5, local copies, waits for them, and re-layouts: 7.7 us -> 5.65 us
where the time goes in v1:
time: 61.1 us; the launch traced here: 59.9 us
  Pallas kernels  53.6 us (88%)
  local copies, waits for them, and re-layouts  5.65 us (9%)
  between operations  0.64 us (1%)
    pallas_call x1, Pallas kernels, body(): pl.pallas_call(functools.partial(kernel, names, owners, slots, 1.0 / math...  53.6 us
    unnamed x5, local copies, waits for them, and re-layouts  5.65 us

profile of v1, /device:TPU:0, one launch (start us, length us, event | category | flops | bytes accessed | tf_op | source)
XLA Modules:
  0.0 59.9 jit_solution(8735885511024398262)
XLA Ops:
  0.6 53.6 %shard_map.76 = (bf16[256,512]{1,0:T(8,128)(2,1)}, bf16[256,4096]{1,0:T(8,128)(2,1)}, bf16[16,128,128]{2,1,0:T(8,128)(2,1)}) custom-call(s32[16]{0:T(128)} %refs_0_.1, f32[16]{0:T(128)} %refs_1_.1, bf16[16,128,128]{2,1,0:T(8,128)(2,1)} %refs_2_.1, bf16[256,4096]{1,0:T(8,128)(2,1)} %refs_3_.1, bf16[256,512]{1,0:T(8,128)(2,1)} %refs_4_.1), custom_call_target="tpu_custom_call" | custom-call | tf_op jit(solution)/shard_map/pallas_call | solution.py:529
  54.3 1.7 %copy.11 = bf16[256,512]{1,0:T(8,128)(2,1)} copy(bf16[256,512]{1,0:T(8,128)(2,1)} %get-tuple-element.6) | data formatting | bytes 524288
  55.9 0.0 copy-start
  55.9 3.2 %copy.12 = bf16[256,4096]{1,0:T(8,128)(2,1)} copy(bf16[256,4096]{1,0:T(8,128)(2,1)} %get-tuple-element.7) | data formatting | bytes 4194304
  59.1 0.0 copy-done
  59.1 0.8 %copy.13 = bf16[16,128,128]{2,1,0:T(8,128)(2,1)} copy(bf16[16,128,128]{2,1,0:T(8,128)(2,1)S(1)} %copy-done) | data formatting | bytes 1048576
Async XLA Ops:
  55.9 3.2 %copy-start = (bf16[16,128,128]{2,1,0:T(8,128)(2,1)S(1)}, bf16[16,128,128]{2,1,0:T(8,128)(2,1)}, u32[]{:S(2)}) copy-start(bf16[16,128,128]{2,1,0:T(8,128)(2,1)} %get-tuple-element.8) | copy-start | bytes 1572868

commit v2 on v1

--- a/solution.py
+++ b/solution.py
@@ -201,9 +201,13 @@
             w_task(d, line_order(d, (j + CHUNKS // 2) % CHUNKS), (behind[d] == 0,))
             w_task(d, line_order(d, j), (p == d, behind[d] > 0))
 
-    def w_secondary(j):
+    def w_middle(j):
         for d in range(2):
-            w_task(d, line_order(d, j), (p == 1 - d,))
+            w_task(d, line_order(d, j), (p == 1 - d, behind[d] < planes - 1))
+
+    def w_end(j):
+        for d in range(2):
+            w_task(d, line_order(d, j), (behind[d] == planes - 1,))
 
     def push(place, k, j):
         return remote(place, place, r.fw_sems.at[0, k, j], r.fw_sems.at[1, k, j], partner)
@@ -213,7 +217,7 @@
 
     def w_final(j):
         q = near_chunk(j)
-        w_secondary(j)
+        w_end(j)
         for i in range(span):
             b = place_block(q, i)
             r.w_all[h, q, y, x, i] = jnp.where(
@@ -358,9 +362,13 @@
             if slot > 0:
                 g_task(d, line_order(d, slot - 1), (p == d, behind[d] > 0))
 
-    def g_secondary(j):
+    def g_middle(j):
         for d in range(2):
-            g_task(d, line_order(d, j), (p == 1 - d,))
+            g_task(d, line_order(d, j), (p == 1 - d, behind[d] < planes - 1))
+
+    def g_final(j):
+        for d in range(2):
+            g_task(d, line_order(d, j), (behind[d] == planes - 1,))
         q = near_chunk(j)
         r.g_full[pl.ds(q * span, span)] = (r.g_plane[q] + behind_sum(0, q) + behind_sum(1, q)).astype(BF16)
 
@@ -421,44 +429,63 @@
     reduce_two(0)
     reduce_one(2)
     w_primary(2)
+    w_middle(0)
     reduce_two(1)
     reduce_one(3)
+    w_primary(3)
     plane_sum(0)
     g_primary(0)
-    w_primary(3)
-    w_final(0)
+    w_middle(1)
     reduce_two(2)
     plane_sum(1)
     g_primary(1)
-    w_final(1)
-    w_forward(0)
+    w_middle(2)
+    w_final(0)
     reduce_two(3)
     plane_sum(2)
     g_primary(2)
+    g_middle(0)
+    w_middle(3)
+    w_final(1)
+    plane_sum(3)
+    g_middle(1)
     w_final(2)
+    w_forward(0)
+    g_primary(3)
+    w_final(3)
     w_forward(1)
     w_diagonal(0)
-    plane_sum(3)
-    g_primary(3)
-    w_final(3)
     g_primary(4)
-    g_secondary(0)
+    products(0)
+    w_diagonal(1)
     w_forward(2)
-    w_diagonal(1)
-    products(0)
-    g_secondary(1)
+    products(1)
+    g_middle(2)
+    g_middle(3)
+    g_final(0)
+    g_final(1)
+    g_final(2)
+    g_final(3)
+    to_owners()
     w_forward(3)
-    g_secondary(2)
-    g_secondary(3)
-    to_owners()
     w_diagonal(2)
-    products(1)
+    products(2)
     w_diagonal(3)
-    products(2)
     finish()
     products(3)
     for end in ends:
         end()
+
+
+def store_kernel(proj, tg, out, proj_h, tg_h, out_h, sems):
+    copies = [
+        pltpu.make_async_copy(src, dst, sems.at[k])
+        for k, (src, dst) in enumerate([(tg, tg_h), (out, out_h), (proj, proj_h)])
+    ]
+    for copy in copies:
+        copy.start()
+    for copy in copies:
+        copy.wait()
 
 
 def body(tokens, block_codes, scales, counts, cotangent):
@@ -526,20 +553,27 @@
         "fp_sems": dma((2, PLANE)),
     }
     names = ["counts_h", "scales_h", "codes_h", "tok_h", "cot_h", "proj", "tg", "out"] + list(scratch)
-    return tuple(pl.pallas_call(
+    shapes = [(local_tokens, key_width), (local_tokens, width), (most, tile, tile)]
+    results = pl.pallas_call(
         functools.partial(kernel, names, owners, slots, 1.0 / math.sqrt(total_tokens)),
         in_specs=[hbm] * 5,
         out_specs=[vmem, vmem, vmem],
-        out_shape=[
-            jax.ShapeDtypeStruct((local_tokens, key_width), BF16),
-            jax.ShapeDtypeStruct((local_tokens, width), BF16),
-            jax.ShapeDtypeStruct((most, tile, tile), BF16),
-        ],
+        out_shape=[pltpu.VMEM(shape, BF16) for shape in shapes],
         scratch_shapes=list(scratch.values()),
         compiler_params=pltpu.CompilerParams(
-            collective_id=0, has_side_effects=True, vmem_limit_bytes=56 * 1024 * 1024
+            collective_id=0, has_side_effects=True, vmem_limit_bytes=44 * 1024 * 1024
         ),
-    )(counts, scales, block_codes, tokens, cotangent))
+    )(*[
+        pltpu.with_memory_space_constraint(v, pltpu.HBM)
+        for v in (counts, scales, block_codes, tokens, cotangent)
+    ])
+    return tuple(pl.pallas_call(
+        store_kernel,
+        in_specs=[vmem] * 3,
+        out_specs=[hbm] * 3,
+        out_shape=[pltpu.HBM(shape, BF16) for shape in shapes],
+        scratch_shapes=[dma((3,))],
+    )(*[pltpu.with_memory_space_constraint(v, pltpu.VMEM) for v in results]))
 
 
 def solution(mesh):

time: 61.1 us -> 53.8 us (0.88); the launches traced: 59.9 us -> 53.6 us
  local copies, waits for them, and re-layouts: 5.65 us -> 0 us
  Pallas kernels: 53.6 us -> 52.9 us
    unnamed x5 -> x0, local copies, waits for them, and re-layouts: 5.65 us -> none
    pallas_call x1, Pallas kernels: 53.6 us -> 51.3 us  [body(): pl.pallas_call(functools.partial(kernel, names, owners, slots, 1.0 / math...]
    pallas_call x0 -> x1, Pallas kernels: none -> 1.59 us  [body(): pl.pallas_call(store_kernel, in_specs=[vmem] * 3, out_specs=[hbm] * 3, ou...]
where the time goes in v2:
time: 53.8 us; the launch traced here: 53.6 us
  Pallas kernels  52.9 us (98%)
  between operations  0.64 us (1%)
    pallas_call x1, Pallas kernels, body(): pl.pallas_call(functools.partial(kernel, names, owners, slots, 1.0 / math...  51.3 us
    pallas_call x1, Pallas kernels, body(): pl.pallas_call(store_kernel, in_specs=[vmem] * 3, out_specs=[hbm] * 3, ou...  1.59 us

profile of v2, /device:TPU:0, one launch (start us, length us, event | category | flops | bytes accessed | tf_op | source)
XLA Modules:
  0.0 53.6 jit_solution(9921618685770803115)
XLA Ops:
  0.6 51.3 %shard_map.76 = (bf16[256,512]{1,0:T(8,128)(2,1)S(1)}, bf16[256,4096]{1,0:T(8,128)(2,1)S(1)}, bf16[16,128,128]{2,1,0:T(8,128)(2,1)S(1)}) custom-call(s32[16]{0:T(128)} %refs_0_.1, f32[16]{0:T(128)} %refs_1_.1, bf16[16,128,128]{2,1,0:T(8,128)(2,1)} %refs_2_.1, bf16[256,4096]{1,0:T(8,128)(2,1)} %refs_3_.1, bf16[256,512]{1,0:T(8,128)(2,1)} %refs_4_.1), custom_call_target="tpu_custom_call" | custom-call | tf_op jit(solution)/shard_map/pallas_call | solution.py:557
  52.0 1.6 %shard_map.77 = (bf16[256,512]{1,0:T(8,128)(2,1)}, bf16[256,4096]{1,0:T(8,128)(2,1)}, bf16[16,128,128]{2,1,0:T(8,128)(2,1)}) custom-call(bf16[256,512]{1,0:T(8,128)(2,1)S(1)} %get-tuple-element.6.proj, bf16[256,4096]{1,0:T(8,128)(2,1)S(1)} %get-tuple-element.7.tg, bf16[16,128,128]{2,1,0:T(8,128)(2,1)S(1)} %get-tuple-element.8.out), custom_call_target="tpu_custom_call" | custom-call | tf_op jit(solution)/shard_map/pallas_call | solution.py:570

commit v3 on v2

--- a/solution.py
+++ b/solution.py
@@ -17,6 +17,7 @@
 CORES = 2
 GROUP = PLANE * CORES
 CHUNKS = 4
+SHARED = (2, 3)
 
 
 def kernel(names, owners, slots, scale, *refs):
@@ -42,6 +43,8 @@
     y_dev = (h, z * PLANE + 2 * oy + x)
     d_dev = (h, z * PLANE + 2 * oy + ox)
     partner = (1 - h, me)
+    shared = SHARED if planes % 4 == 0 and part % 2 == 0 else ()
+    pair_dev = (h, (z + 1 - 2 * (z % 2)) * PLANE + c)
 
     def z_dev(d):
         return (h, ((z + 1 - 2 * d + planes) % planes) * PLANE + c)
@@ -223,27 +226,50 @@
             r.w_all[h, q, y, x, i] = jnp.where(
                 b < base, r.w_recv[0, q, i], jnp.where(b >= plane_end, r.w_recv[1, q, i], r.own_v[q, i])
             )
-        place = r.w_all.at[h, q, y, x]
+        place = r.w_all.at[h, q, y, x, gathered(j)]
         go(gather_copy(place, 0, j, x_dev))
         go(gather_copy(place, 1, j, y_dev))
-        go(push(place, 0, j))
+        go(push(r.w_all.at[h, q, y, x], 0, j))
+
+    def gathered(j, half=None, other=False):
+        start, size = 0, span
+        if j in shared:
+            size = part
+            start = ((1 - z % 2) if other else z % 2) * part
+        if half is not None:
+            size = size // 2
+            start = start + half * size
+        return pl.ds(start, size)
 
     def w_forward(j):
         q = near_chunk(j)
-        place = r.w_all.at[h, q, y, ox]
-        gather_copy(place, 0, j, x_dev).wait_recv()
-        go(gather_copy(r.w_all.at[h, q, y, ox, first], 2, j, y_dev))
-        go(push(place, 1, j))
-        place = r.w_all.at[h, q, oy, x]
-        gather_copy(place, 1, j, y_dev).wait_recv()
-        go(gather_copy(r.w_all.at[h, q, oy, x, last], 3, j, x_dev))
-        go(push(place, 2, j))
+        for k, (ty, tx) in ((1, (y, ox)), (2, (oy, x))):
+            source, device = ((x_dev, y_dev), (y_dev, x_dev))[k - 1]
+            place = r.w_all.at[h, q, ty, tx, gathered(j)]
+            gather_copy(place, k - 1, j, source).wait_recv()
+            go(gather_copy(r.w_all.at[h, q, ty, tx, gathered(j, k - 1)], k + 1, j, device))
+            if j in shared:
+                go(gather_copy(place, 3 + k, j, pair_dev))
+            else:
+                go(push(place, k, j))
 
     def w_diagonal(j):
         q = near_chunk(j)
-        gather_copy(r.w_all.at[h, q, oy, ox, first], 2, j, y_dev).wait_recv()
-        gather_copy(r.w_all.at[h, q, oy, ox, last], 3, j, x_dev).wait_recv()
-        go(push(r.w_all.at[h, q, oy, ox], 3, j))
+        gather_copy(r.w_all.at[h, q, oy, ox, gathered(j, 0)], 2, j, y_dev).wait_recv()
+        gather_copy(r.w_all.at[h, q, oy, ox, gathered(j, 1)], 3, j, x_dev).wait_recv()
+        place = r.w_all.at[h, q, oy, ox, gathered(j)]
+        if j in shared:
+            go(gather_copy(place, 6, j, pair_dev))
+        else:
+            go(push(place, 3, j))
+
+    def w_paired(j):
+        q = near_chunk(j)
+        if j in shared:
+            for k in range(1, PLANE):
+                ty, tx = mates[k]
+                gather_copy(r.w_all.at[h, q, ty, tx, gathered(j, other=True)], 3 + k, j, pair_dev).wait_recv()
+                go(push(r.w_all.at[h, q, ty, tx], k, j))
 
     depth = r.w_mat.shape[0]
     row_tiles = depth // tile
@@ -355,12 +381,13 @@
         guarded(sends, add)
         go(copy, sends)
 
-    def g_primary(slot):
+    def g_first(j):
         for d in range(2):
-            if slot < CHUNKS:
-                g_task(d, line_order(d, slot), (behind[d] == 0,))
-            if slot > 0:
-                g_task(d, line_order(d, slot - 1), (p == d, behind[d] > 0))
+            g_task(d, line_order(d, j), (behind[d] == 0,))
+
+    def g_next(j):
+        for d in range(2):
+            g_task(d, line_order(d, j), (p == d, behind[d] > 0))
 
     def g_middle(j):
         for d in range(2):
@@ -396,10 +423,12 @@
             go(owner_copy(k))
         go(give(0))
 
-    def finish():
+    def share_owned():
         for k in (1, 2, 3):
             owner_copy(k).wait_recv()
             go(give(k))
+
+    def finish():
         for k in range(PLANE):
             ty, tx = mates[k]
             place = r.fs_all.at[1 - h, 2 * ty + tx]
@@ -434,43 +463,51 @@
     reduce_one(3)
     w_primary(3)
     plane_sum(0)
-    g_primary(0)
+    g_first(0)
     w_middle(1)
     reduce_two(2)
+    w_middle(2)
     plane_sum(1)
-    g_primary(1)
-    w_middle(2)
+    g_first(1)
+    g_next(0)
+    w_middle(3)
+    reduce_two(3)
     w_final(0)
-    reduce_two(3)
+    w_final(1)
     plane_sum(2)
-    g_primary(2)
+    g_first(2)
+    g_next(1)
     g_middle(0)
-    w_middle(3)
-    w_final(1)
     plane_sum(3)
+    g_first(3)
+    w_final(2)
+    w_final(3)
+    w_forward(0)
+    g_next(2)
     g_middle(1)
-    w_final(2)
-    w_forward(0)
-    g_primary(3)
-    w_final(3)
     w_forward(1)
+    g_next(3)
+    w_forward(2)
+    w_forward(3)
     w_diagonal(0)
-    g_primary(4)
-    products(0)
+    g_middle(2)
     w_diagonal(1)
-    w_forward(2)
-    products(1)
-    g_middle(2)
     g_middle(3)
     g_final(0)
     g_final(1)
     g_final(2)
     g_final(3)
     to_owners()
-    w_forward(3)
     w_diagonal(2)
+    w_paired(0)
+    products(0)
+    w_diagonal(3)
+    w_paired(1)
+    products(1)
+    w_paired(2)
+    share_owned()
+    w_paired(3)
     products(2)
-    w_diagonal(3)
     finish()
     products(3)
     for end in ends:
@@ -544,7 +581,7 @@
         "tok_sems": dma((CHUNKS,)),
         "sc_sems": dma((2, PLANE)),
         "wz_sems": dma((2, 2, CHUNKS)),
-        "ag_sems": dma((2, 4, CHUNKS)),
+        "ag_sems": dma((2, 7, CHUNKS)),
         "fw_sems": dma((2, 4, CHUNKS)),
         "pair_sems": dma((2, CHUNKS)),
         "rs_sems": dma((2, 4, CHUNKS)),

time: 53.8 us -> 49.7 us (0.924)
  Pallas kernels: 52.9 us -> 48.7 us
    pallas_call x1, Pallas kernels: 51.3 us -> 47.1 us  [body(): pl.pallas_call(functools.partial(kernel, names, owners, slots, 1.0 / math...]
where the time goes in v3:
time: 49.7 us; the launch traced here: 49.4 us
  Pallas kernels  48.7 us (98%)
  between operations  0.64 us (1%)
    pallas_call x1, Pallas kernels, body(): pl.pallas_call(functools.partial(kernel, names, owners, slots, 1.0 / math...  47.1 us
    pallas_call x1, Pallas kernels, body(): pl.pallas_call(store_kernel, in_specs=[vmem] * 3, out_specs=[hbm] * 3, ou...  1.59 us

profile of v3, /device:TPU:0, one launch (start us, length us, event | category | flops | bytes accessed | tf_op | source)
XLA Modules:
  0.0 49.4 jit_solution(8743475120588589894)
XLA Ops:
  0.6 47.1 %shard_map.76 = (bf16[256,512]{1,0:T(8,128)(2,1)S(1)}, bf16[256,4096]{1,0:T(8,128)(2,1)S(1)}, bf16[16,128,128]{2,1,0:T(8,128)(2,1)S(1)}) custom-call(s32[16]{0:T(128)} %refs_0_.1, f32[16]{0:T(128)} %refs_1_.1, bf16[16,128,128]{2,1,0:T(8,128)(2,1)} %refs_2_.1, bf16[256,4096]{1,0:T(8,128)(2,1)} %refs_3_.1, bf16[256,512]{1,0:T(8,128)(2,1)} %refs_4_.1), custom_call_target="tpu_custom_call" | custom-call | tf_op jit(solution)/shard_map/pallas_call | solution.py:594
  47.8 1.6 %shard_map.77 = (bf16[256,512]{1,0:T(8,128)(2,1)}, bf16[256,4096]{1,0:T(8,128)(2,1)}, bf16[16,128,128]{2,1,0:T(8,128)(2,1)}) custom-call(bf16[256,512]{1,0:T(8,128)(2,1)S(1)} %get-tuple-element.6.proj, bf16[256,4096]{1,0:T(8,128)(2,1)S(1)} %get-tuple-element.7.tg, bf16[16,128,128]{2,1,0:T(8,128)(2,1)S(1)} %get-tuple-element.8.out), custom_call_target="tpu_custom_call" | custom-call | tf_op jit(solution)/shard_map/pallas_call | solution.py:607

commit v4 on v3

--- a/solution.py
+++ b/solution.py
@@ -250,8 +250,7 @@
             go(gather_copy(r.w_all.at[h, q, ty, tx, gathered(j, k - 1)], k + 1, j, device))
             if j in shared:
                 go(gather_copy(place, 3 + k, j, pair_dev))
-            else:
-                go(push(place, k, j))
+            go(push(place, k, j))
 
     def w_diagonal(j):
         q = near_chunk(j)
@@ -260,40 +259,48 @@
         place = r.w_all.at[h, q, oy, ox, gathered(j)]
         if j in shared:
             go(gather_copy(place, 6, j, pair_dev))
-        else:
-            go(push(place, 3, j))
+        go(push(place, 3, j))
 
     def w_paired(j):
         q = near_chunk(j)
         if j in shared:
             for k in range(1, PLANE):
                 ty, tx = mates[k]
-                gather_copy(r.w_all.at[h, q, ty, tx, gathered(j, other=True)], 3 + k, j, pair_dev).wait_recv()
-                go(push(r.w_all.at[h, q, ty, tx], k, j))
+                place = r.w_all.at[h, q, ty, tx, gathered(j, other=True)]
+                gather_copy(place, 3 + k, j, pair_dev).wait_recv()
+                go(push(place, 3 + k, j))
 
     depth = r.w_mat.shape[0]
     row_tiles = depth // tile
 
     def products(j):
         q = near_chunk(j)
-        for k, (ty, tx) in enumerate(mates):
-            push(r.w_all.at[1 - h, q, ty, tx], k, j).wait_recv()
+        push(r.w_all.at[1 - h, q, y, x], 0, j).wait_recv()
+        for k in range(1, PLANE):
+            ty, tx = mates[k]
+            push(r.w_all.at[1 - h, q, ty, tx, gathered(j)], k, j).wait_recv()
+            if j in shared:
+                push(r.w_all.at[1 - h, q, ty, tx, gathered(j, other=True)], 3 + k, j).wait_recv()
         for rr in range(row_tiles):
             for cc in range(PLANE):
                 r.w_mat[rr * tile : (rr + 1) * tile, cc * tile : (cc + 1) * tile] = r.w_all[
                     rr % CORES, q, cc // 2, cc % 2, rr // CORES
                 ]
+        if j == CHUNKS - 1:
+            return
         weight = r.w_mat[...]
         term = jnp.dot(r.tok_v[q], weight, preferred_element_type=F32)
         if j == 0:
             r.acc[...] = term
-        elif j < CHUNKS - 1:
+        else:
             r.acc[...] += term
-        else:
-            r.proj[...] = (r.acc[...] + term).astype(BF16)
         r.tg[:, pl.ds(pl.multiple_of(q * depth, depth), depth)] = lax.dot_general(
             r.cot_v[...], weight, (((1,), (1,)), ((), ())), preferred_element_type=F32
         ).astype(BF16)
+
+    def keep_last():
+        r.tok_last[...] = r.tok_v[near_chunk(CHUNKS - 1)]
+        r.cot_last[...] = r.cot_v[...]
 
     steps = 2
     sub = depth // steps
@@ -450,11 +457,11 @@
     reduce_one(0)
     pair_sum(1)
     reduce_one(1)
+    pair_sum(2)
+    pair_sum(3)
     gather_own()
     w_primary(0)
     w_primary(1)
-    pair_sum(2)
-    pair_sum(3)
     reduce_two(0)
     reduce_one(2)
     w_primary(2)
@@ -482,6 +489,7 @@
     g_first(3)
     w_final(2)
     w_final(3)
+    keep_last()
     w_forward(0)
     g_next(2)
     g_middle(1)
@@ -489,15 +497,15 @@
     g_next(3)
     w_forward(2)
     w_forward(3)
-    w_diagonal(0)
     g_middle(2)
-    w_diagonal(1)
     g_middle(3)
     g_final(0)
     g_final(1)
     g_final(2)
     g_final(3)
     to_owners()
+    w_diagonal(0)
+    w_diagonal(1)
     w_diagonal(2)
     w_paired(0)
     products(0)
@@ -514,13 +522,29 @@
         end()
 
 
-def store_kernel(proj, tg, out, proj_h, tg_h, out_h, sems):
-    copies = [
-        pltpu.make_async_copy(src, dst, sems.at[k])
-        for k, (src, dst) in enumerate([(tg, tg_h), (out, out_h), (proj, proj_h)])
-    ]
+def last_kernel(planes, acc, tg, out, w_mat, tok_last, cot_last, proj_h, tg_h, out_h, proj_v, tail_v, sems):
+    depth = w_mat.shape[0]
+    p = (2 * (lax.axis_index("fsdp") // PLANE)) // planes
+    q = (CHUNKS - 1 + (CHUNKS // 2) * p) % CHUNKS
+
+    def columns(chunk):
+        return pl.ds(pl.multiple_of(chunk * depth, depth), depth)
+
+    copies = [pltpu.make_async_copy(out, out_h, sems.at[0])]
+    for k in range(1, CHUNKS):
+        place = columns((q + k) % CHUNKS)
+        copies.append(pltpu.make_async_copy(tg.at[:, place], tg_h.at[:, place], sems.at[k]))
     for copy in copies:
         copy.start()
+    weight = w_mat[...]
+    tail_v[...] = lax.dot_general(
+        cot_last[...], weight, (((1,), (1,)), ((), ())), preferred_element_type=F32
+    ).astype(BF16)
+    copies.append(pltpu.make_async_copy(tail_v, tg_h.at[:, columns(q)], sems.at[CHUNKS]))
+    copies[-1].start()
+    proj_v[...] = (acc[...] + jnp.dot(tok_last[...], weight, preferred_element_type=F32)).astype(BF16)
+    copies.append(pltpu.make_async_copy(proj_v, proj_h, sems.at[CHUNKS + 1]))
+    copies[-1].start()
     for copy in copies:
         copy.wait()
 
@@ -560,8 +584,6 @@
         "w_send": held(2, CHUNKS, span),
         "w_recv": held(2, CHUNKS, span),
         "w_all": held(CORES, CHUNKS, 2, 2, span),
-        "w_mat": pltpu.VMEM((depth, key_width), BF16),
-        "acc": pltpu.VMEM((local_tokens, key_width), F32),
         "g_terms": held(CORES, CHUNKS, 2, 2, span),
         "g_pair": held(CHUNKS, 2, 2, span),
         "g_sum": held(CHUNKS, 2, 2, span),
@@ -582,20 +604,25 @@
         "sc_sems": dma((2, PLANE)),
         "wz_sems": dma((2, 2, CHUNKS)),
         "ag_sems": dma((2, 7, CHUNKS)),
-        "fw_sems": dma((2, 4, CHUNKS)),
+        "fw_sems": dma((2, 7, CHUNKS)),
         "pair_sems": dma((2, CHUNKS)),
         "rs_sems": dma((2, 4, CHUNKS)),
         "gz_sems": dma((2, 2, CHUNKS)),
         "fs_sems": dma((2, PLANE)),
         "fp_sems": dma((2, PLANE)),
     }
-    names = ["counts_h", "scales_h", "codes_h", "tok_h", "cot_h", "proj", "tg", "out"] + list(scratch)
+    names = ["counts_h", "scales_h", "codes_h", "tok_h", "cot_h", "acc", "tg", "out", "w_mat", "tok_last", "cot_last"] + list(scratch)
     shapes = [(local_tokens, key_width), (local_tokens, width), (most, tile, tile)]
+    planes = owners // PLANE
+    kept = [pltpu.VMEM(shapes[0], F32)] + [
+        pltpu.VMEM(shape, BF16)
+        for shape in shapes[1:] + [(depth, key_width), (local_tokens, depth), (local_tokens, key_width)]
+    ]
     results = pl.pallas_call(
         functools.partial(kernel, names, owners, slots, 1.0 / math.sqrt(total_tokens)),
         in_specs=[hbm] * 5,
-        out_specs=[vmem, vmem, vmem],
-        out_shape=[pltpu.VMEM(shape, BF16) for shape in shapes],
+        out_specs=[vmem] * len(kept),
+        out_shape=kept,
         scratch_shapes=list(scratch.values()),
         compiler_params=pltpu.CompilerParams(
             collective_id=0, has_side_effects=True, vmem_limit_bytes=44 * 1024 * 1024
@@ -605,11 +632,14 @@
         for v in (counts, scales, block_codes, tokens, cotangent)
     ])
     return tuple(pl.pallas_call(
-        store_kernel,
-        in_specs=[vmem] * 3,
+        functools.partial(last_kernel, planes),
+        in_specs=[vmem] * len(kept),
         out_specs=[hbm] * 3,
         out_shape=[pltpu.HBM(shape, BF16) for shape in shapes],
-        scratch_shapes=[dma((3,))],
+        scratch_shapes=[
+            pltpu.VMEM(shapes[0], BF16), pltpu.VMEM((local_tokens, depth), BF16), dma((CHUNKS + 2,))
+        ],
+        compiler_params=pltpu.CompilerParams(vmem_limit_bytes=16 * 1024 * 1024),
     )(*[pltpu.with_memory_space_constraint(v, pltpu.VMEM) for v in results]))
 
 

time: 49.7 us -> 49.6 us (level)
    pallas_call x1, Pallas kernels: 1.59 us -> 2.16 us  [body(): pl.pallas_call(functools.partial(last_kernel, planes), in_specs=[vmem] *...]
    pallas_call x1, Pallas kernels: 47.1 us -> 46.6 us  [body(): pl.pallas_call(functools.partial(kernel, names, owners, slots, 1.0 / math...]
where the time goes in v4:
time: 49.6 us; the launch traced here: 49.4 us
  Pallas kernels  48.8 us (98%)
  between operations  0.64 us (1%)
    pallas_call x1, Pallas kernels, body(): pl.pallas_call(functools.partial(kernel, names, owners, slots, 1.0 / math...  46.6 us
    pallas_call x1, Pallas kernels, body(): pl.pallas_call(functools.partial(last_kernel, planes), in_specs=[vmem] *...  2.16 us

profile of v4, /device:TPU:0, one launch (start us, length us, event | category | flops | bytes accessed | tf_op | source)
XLA Modules:
  0.0 49.4 jit_solution(9517905610417752010)
XLA Ops:
  0.6 46.6 %shard_map.76 = (f32[256,512]{1,0:T(8,128)S(1)}, bf16[256,4096]{1,0:T(8,128)(2,1)S(1)}, bf16[16,128,128]{2,1,0:T(8,128)(2,1)S(1)}, bf16[1024,512]{1,0:T(8,128)(2...) custom-call(s32[16]{0:T(128)} %refs_0_.1, f32[16]{0:T(128)} %refs_1_.1, ...), custom_call_target="tpu_custom_call" | custom-call | tf_op jit(solution)/shard_map/pallas_call | solution.py:621
  47.2 2.2 %shard_map.77 = (bf16[256,512]{1,0:T(8,128)(2,1)}, bf16[256,4096]{1,0:T(8,128)(2,1)}, bf16[16,128,128]{2,1,0:T(8,128)(2,1)}) custom-call(f32[256,512]{1,0:T(8,128)S(1)} %get-tuple-element.9.acc, bf16[256,4096]{1,0:T(8,128)(2,1)S(1)} %get-tuple-element.10.tg, bf16[16,128,128]{2,1,0:T(8,128)(2,1)S(1)} %get-tuple-element.11.out, ...), custom_call_target="tpu_custom_call" | custom-call | tf_op jit(solution)/shard_map/pallas_call | solution.py:634
